TPU v7x, 256 devices: a whole 4x4x8 slice. The times are simulated.
256 devices in a mesh: rep: 32 (over x_hi, z, core), tp: 8 (over x_lo, y).
Axes of the slice: x: 4 (x_hi: 2, x_lo: 2; x = x_hi * 2 + x_lo), y: 4, z: 8, core: 2. Of those that a mesh axis runs over, the one named last changes fastest.
Arguments:
- tokens: bfloat16 [32, 1024, 3072], P('rep', 'tp'), may hold values from -100 to 100
- norm_gain: float32 [32, 3072], P('rep'), may hold values from 0.5 to 1.5
- w_query: bfloat16 [32, 3072, 2048], P('rep', None, 'tp'), may hold values from -1 to 1
- key_weight: bfloat16 [32, 3072, 1024], P('rep', None, 'tp'), may hold values from -1 to 1
- value_weight: bfloat16 [32, 3072, 1024], P('rep', None, 'tp'), may hold values from -0.109375 to 0.109375
- attention_gradient: bfloat16 [32, 1024, 2048], P('rep', None, 'tp'), may hold values from -6 to 6
- global_fragment: float32 [512, 3072], P('tp'), may hold values from -6 to 6
- momentum: float32 [512, 3072], P('tp'), may hold values from -3 to 3
- local_fragment: bfloat16 [32, 512, 3072], P('rep', 'tp'), may hold values from -6 to 6
Outputs:
- grad_query_w: bfloat16 [32, 3072, 2048], P('rep', None, 'tp')
- grad_key_w: bfloat16 [32, 3072, 1024], P('rep', None, 'tp')
- grad_value_w: bfloat16 [32, 3072, 1024], P('rep', None, 'tp')
- grad_gain: float32 [32, 3072], P('rep')
- grad_tokens: bfloat16 [32, 1024, 3072], P('rep', 'tp')
- new_global: float32 [512, 3072], P('tp')
- new_momentum: float32 [512, 3072], P('tp')
All inputs are finite; a program needn't handle non-finite values.
Results may differ from a plain program's by a relative error of at most 0.019.
The roundings to bfloat16 on the way count: a program that leaves them out, or rounds other values in their place, can miss the bound.
Values may be sent and summed in bfloat16 or wider, within the bound.
No kernel may reach another device: no remote copies, remote signals or barrier semaphores. Data moves between devices by JAX's collectives and lax.ppermute only.
A program may use at most 128 MiB of HBM per device.

v0:
```python
import jax
import jax.numpy as jnp
from jax import lax
from jax.sharding import PartitionSpec as P

HEAD_SIZE = 128
epsilon = 1e-05
rope_base = 500000.0
outer_rate = 0.7
outer_momentum = 0.9


def sent_to_all(value, axis):
    copies = jnp.broadcast_to(value, (lax.axis_size(axis), *value.shape))
    return lax.all_to_all(copies, axis, split_axis=0, concat_axis=0, tiled=True)


def of_everyone(value, axis):
    everything = sent_to_all(value, axis)
    return jnp.sum(everything, axis=0)


def cut_along(value, dim, size):
    before, after = (value.shape[:dim], value.shape[dim + 1 :])
    return jnp.moveaxis(value.reshape(*before, size, -1, *after), dim, 0)


def sent_and_summed(value, axis, dim):
    parts = cut_along(value, dim, lax.axis_size(axis))
    arrived = lax.all_to_all(parts, axis, split_axis=0, concat_axis=0, tiled=True)
    return arrived.sum(axis=0)


def in_one_piece(arrays, axis, dim, along):
    both = jnp.concatenate(arrays, axis=along)
    whole, at, done = (lax.all_gather(both, axis, axis=dim, tiled=True), 0, [])
    for a in arrays:
        done.append(lax.slice_in_dim(whole, at, at + a.shape[along], axis=along))
        at += a.shape[along]
    return tuple(done)


def rope_tables(sequence_length, width):
    middle = width // 2
    frequency = rope_base ** (-2.0 * jnp.arange(middle, dtype=jnp.float32) / width)
    angles = jnp.arange(sequence_length, dtype=jnp.float32)[:, None] * frequency[None, :]
    angles = jnp.concatenate([angles, angles], axis=1)
    return (jnp.cos(angles)[:, None, :], jnp.sin(angles)[:, None, :])


def rotate(vectors, cosine_table, sine_table):
    middle = vectors.shape[-1] // 2
    turned = jnp.concatenate([-vectors[..., middle:], vectors[..., :middle]], axis=-1)
    return vectors * cosine_table + turned * sine_table


def reverse_rotation(gradient, cosine_table, sine_table):
    middle = gradient.shape[-1] // 2
    shifted = gradient * sine_table
    turned = jnp.concatenate([shifted[..., middle:], -shifted[..., :middle]], axis=-1)
    return gradient * cosine_table + turned


def attention_reverse(query_rows, rotated_keys, values_bfloat, grad_out, block_of_rows):
    sequence_length = query_rows.shape[0]
    score_scale = query_rows.shape[-1] ** (-0.5)

    def one_block(running, block_index):
        acc_key, acc_value = running
        offset = block_index * block_of_rows
        query_block = lax.dynamic_slice_in_dim(query_rows, offset, block_of_rows, 0)
        grad_block = lax.dynamic_slice_in_dim(grad_out, offset, block_of_rows, 0)
        scores = (
            jnp.einsum(
                "qgrd,kgd->grqk", query_block, rotated_keys, preferred_element_type=jnp.float32
            )
            * score_scale
        )
        row_pos = offset + jnp.arange(block_of_rows)
        col_pos = jnp.arange(sequence_length)
        allowed = col_pos[None, :] <= row_pos[:, None]
        scores = jnp.where(allowed, scores, -jnp.inf)
        highest = jnp.max(scores, axis=-1, keepdims=True)
        powers = jnp.exp(scores - highest)
        probability = powers / jnp.sum(powers, axis=-1, keepdims=True)
        prob_low = probability.astype(jnp.bfloat16)
        acc_value = acc_value + jnp.einsum(
            "grqk,qgrd->kgd", prob_low, grad_block, preferred_element_type=jnp.float32
        )
        grad_prob = jnp.einsum(
            "qgrd,kgd->grqk", grad_block, values_bfloat, preferred_element_type=jnp.float32
        )
        grad_score = (
            probability
            * (grad_prob - jnp.sum(grad_prob * probability, axis=-1, keepdims=True))
            * score_scale
        )
        score_low = grad_score.astype(jnp.bfloat16)
        grad_query = jnp.einsum(
            "grqk,kgd->qgrd", score_low, rotated_keys, preferred_element_type=jnp.float32
        )
        acc_key = acc_key + jnp.einsum(
            "grqk,qgrd->kgd", score_low, query_block, preferred_element_type=jnp.float32
        )
        return ((acc_key, acc_value), grad_query)

    initial = jnp.zeros(rotated_keys.shape, jnp.float32)
    (acc_key, acc_value), grad_blocks = lax.scan(
        one_block, (initial, initial), jnp.arange(sequence_length // block_of_rows)
    )
    return (grad_blocks.reshape(query_rows.shape), acc_key, acc_value)


def body(
    tokens,
    norm_gain,
    w_query,
    key_weight,
    value_weight,
    attention_gradient,
    global_fragment,
    momentum,
    local_fragment,
):
    local_rows = tokens[0]
    norm_gains = norm_gain[0]
    weight_q = w_query[0]
    weight_k = key_weight[0]
    weight_v = value_weight[0]
    widened_rows = local_rows.astype(jnp.float32)
    inverse_norm = lax.rsqrt(
        jnp.mean(widened_rows * widened_rows, axis=-1, keepdims=True) + epsilon
    )
    normalized_input = widened_rows * inverse_norm
    normalized_local = (normalized_input * norm_gains[None, :]).astype(jnp.bfloat16)
    normalized = lax.all_gather(normalized_local, "tp", axis=0, tiled=True)
    sequence_length = normalized.shape[0]
    heads_q = weight_q.shape[1] // HEAD_SIZE
    heads_kv = weight_k.shape[1] // HEAD_SIZE
    cosine_table, sine_table = rope_tables(sequence_length, HEAD_SIZE)
    query_rows = jnp.dot(normalized, weight_q, preferred_element_type=jnp.float32).reshape(
        sequence_length, heads_q, HEAD_SIZE
    )
    query_rows = rotate(query_rows, cosine_table, sine_table).astype(jnp.bfloat16)
    rotated_keys = jnp.dot(normalized, weight_k, preferred_element_type=jnp.float32).reshape(
        sequence_length, heads_kv, HEAD_SIZE
    )
    rotated_keys = rotate(rotated_keys, cosine_table, sine_table).astype(jnp.bfloat16)
    values_bfloat = (
        jnp.dot(normalized, weight_v, preferred_element_type=jnp.float32)
        .astype(jnp.bfloat16)
        .reshape(sequence_length, heads_kv, HEAD_SIZE)
    )
    replica_group = heads_q // heads_kv
    block_of_rows = min(512, sequence_length)
    query_input_gradient, key_input_gradient, value_input_gradient = attention_reverse(
        query_rows.reshape(sequence_length, heads_kv, replica_group, HEAD_SIZE),
        rotated_keys,
        values_bfloat,
        attention_gradient[0].reshape(sequence_length, heads_kv, replica_group, HEAD_SIZE),
        block_of_rows,
    )
    dquery = (
        reverse_rotation(
            query_input_gradient.reshape(sequence_length, heads_q, HEAD_SIZE),
            cosine_table,
            sine_table,
        )
        .astype(jnp.bfloat16)
        .reshape(sequence_length, heads_q * HEAD_SIZE)
    )
    key_gradient = (
        reverse_rotation(key_input_gradient, cosine_table, sine_table)
        .astype(jnp.bfloat16)
        .reshape(sequence_length, heads_kv * HEAD_SIZE)
    )
    value_gradient = value_input_gradient.astype(jnp.bfloat16).reshape(
        sequence_length, heads_kv * HEAD_SIZE
    )
    contract = (((0,), (0,)), ((), ()))
    grad_wq = lax.dot_general(
        normalized, dquery, contract, preferred_element_type=jnp.float32
    ).astype(jnp.bfloat16)
    grad_wk = lax.dot_general(
        normalized, key_gradient, contract, preferred_element_type=jnp.float32
    ).astype(jnp.bfloat16)
    grad_wv = lax.dot_general(
        normalized, value_gradient, contract, preferred_element_type=jnp.float32
    ).astype(jnp.bfloat16)
    back = (((1,), (1,)), ((), ()))
    partial_value = lax.dot_general(dquery, weight_q, back, preferred_element_type=jnp.float32)
    partial_value = partial_value + lax.dot_general(
        key_gradient, weight_k, back, preferred_element_type=jnp.float32
    )
    summed_rows = lax.psum_scatter(
        (
            partial_value
            + lax.dot_general(value_gradient, weight_v, back, preferred_element_type=jnp.float32)
        ).astype(jnp.bfloat16),
        "tp",
        scatter_dimension=0,
        tiled=True,
    ).astype(jnp.float32)
    gains_gradient = of_everyone(jnp.sum(summed_rows * normalized_input, axis=0), "tp")
    scaled_rows = summed_rows * norm_gains[None, :]
    gradient_rows = (
        inverse_norm
        * (
            scaled_rows
            - normalized_input * jnp.mean(scaled_rows * normalized_input, axis=-1, keepdims=True)
        )
    ).astype(jnp.bfloat16)
    delta = global_fragment - local_fragment[0].astype(jnp.float32)
    replicas = lax.axis_size("rep")
    delta_rows = sent_and_summed(delta, "rep", 0) / replicas
    row_count = delta_rows.shape[0]
    offset = lax.axis_index("rep") * row_count
    momentum_rows = lax.dynamic_slice_in_dim(momentum, offset, row_count, 0)
    global_rows = lax.dynamic_slice_in_dim(global_fragment, offset, row_count, 0)
    momentum_next = outer_momentum * momentum_rows + delta_rows
    global_next = global_rows - outer_rate * (delta_rows + outer_momentum * momentum_next)
    new_global, new_momentum = in_one_piece((global_next, momentum_next), "rep", 0, 1)
    return (
        grad_wq[None],
        grad_wk[None],
        grad_wv[None],
        gains_gradient[None],
        gradient_rows[None],
        new_global,
        new_momentum,
    )


def solution(mesh):
    placed = (
        P("rep", "tp", None),
        P("rep", None),
        P("rep", None, "tp"),
        P("rep", None, "tp"),
        P("rep", None, "tp"),
        P("rep", None, "tp"),
        P("tp", None),
        P("tp", None),
        P("rep", "tp", None),
    )
    return jax.shard_map(
        body,
        mesh=mesh,
        in_specs=placed,
        out_specs=(
            P("rep", None, "tp"),
            P("rep", None, "tp"),
            P("rep", None, "tp"),
            P("rep", None),
            P("rep", "tp", None),
            P("tp", None),
            P("tp", None),
        ),
        check_vma=False,
    )
```

profile of v0, /device:TPU:4, one launch (start us, length us, event | category | flops | bytes accessed | tf_op | source)
XLA Modules:
  0.0 287.7 jit_solution(629735918191153067)
XLA Ops:
  7.2 1.5 fusion.54
  9.3 2.3 fusion.51
  11.6 1.3 convert_subtract_fusion
  12.9 1.3 reshape.228
  14.2 11.6 %all-to-all-start.1 = ((f32[32,2,3072]{2,1,0:T(2,128)}), f32[32,2,3072]{2,1,0:T(2,128)S(1)}, u32[]{:S(2)}, u32[]{:S(2)}) async-start(f32[32,2,3072]{2,1,0:T(2,128)} %reshape.228), calls=%async_computation.2 | async-start | bytes 1572864 | tf_op jit(solution)/shard_map/all_to_all | solution.py:30
  25.9 1.7 copy.69
  27.7 2.0 copy.58
  30.6 17.6 %all-to-all-done.1 = f32[32,2,3072]{2,1,0:T(2,128)S(1)} async-done(((f32[32,2,3072]{2,1,0:T(2,128)}), f32[32,2,3072]{2,1,0:T(2,128)S(1)}, u32[]{:S(2)}, u32[]{:S(2)}) %all-to-all-start.1) | async-done | bytes 786464 | tf_op jit(solution)/shard_map/all_to_all | solution.py:30
  50.1 47.4 %all-gather.4.cloned.1.call-done = bf16[1024,3072]{1,0:T(8,128)(2,1)} async-done(((bf16[128,3072]{1,0:T(8,128)(2,1)}), bf16[1024,3072]{1,0:T(8,128)(2,1)}) %all-gather.4.cloned.1.call-update) | async-done | bytes 6291472 | tf_op jit(solution)/shard_map/all_gather | solution.py:136
  97.5 5.2 %fusion.39 = f32[1024,2,128]{0,2,1:T(8,128)S(1)} fusion(bf16[2,128,3072]{2,1,0:T(8,128)(2,1)} %bitcast.242, bf16[1024,3072]{1,0:T(8,128)(2,1)} %all-gather.4.cloned.1.call-done), kind=kOutput, calls=%fused_computation.43 | convolution fusion | flops 1610612736 | bytes 8912896 | tf_op jit(solution)/shard_map/dot_general | solution.py:141
  103.6 2.2 fusion.67
  105.9 2.9 %fusion.81 = (bf16[1024,1,128]{0,2,1:T(8,128)(2,1)}, f32[1024,128]{0,1:T(8,128)S(1)}, f32[1024,128]{0,1:T(8,128)S(1)}) fusion(f32[1024,64]{0,1:T(8,128)S(1)} %get-tuple-element.171, f32[1024,64]{0,1:T(8,128)S(1)} %get-tuple-element.170, f32[1024,128]{0,1:T(8,128)S(1)} %fusion.67, f32[1024,64]{0,1:T(8,128)S(1)} %copy-done.15), kind=kLoop, calls=%fused_computation.102 | loop fusion | flops 786432 | bytes 2621440 | tf_op jit(solution)/shard_map/convert_element_type | solution.py:148
  108.8 2.0 copy.60
  110.8 2.2 fusion.69
  113.0 5.4 %fusion.57 = bf16[1024,1,128]{2,0,1:T(8,128)(2,1)} fusion(bf16[1024,3072]{1,0:T(8,128)(2,1)} %all-gather.4.cloned.1.call-done, bf16[1,3072,128]{2,1,0:T(8,128)(2,1)} %param.15), kind=kOutput, calls=%fused_computation.68 | convolution fusion | flops 805437440 | bytes 7340032 | tf_op jit(solution)/shard_map/dot_general | solution.py:150
  118.4 39.0 %while.15 = (s32[]{:T(128)}, f32[1024,1,128]{0,2,1:T(8,128)}, f32[1024,1,128]{0,2,1:T(8,128)}, f32[2,512,1,2,128]{4,1,3,2,0:T(8,128)}, s32[2]{0:T(128)S(1)}, /*i...) while((s32[]{:T(128)}, f32[1024,1,128]{0,2,1:T(8,128)}, ...), condition=%wide.region_5.6_spmd.clone, body=%wide.region_1.5_spmd.clone.sunk | while | flops 1370486272 | bytes 68469048 | solution.py:108
  120.0 2.1 fusion.121
  123.3 3.3 %fusion.123 = (f32[2,512]{1,0:T(2,128)S(1)}, f32[512,2,1024]{2,0,1:T(8,128)S(1)}) fusion(f32[2,512]{1,0:T(2,128)S(1)} %fusion.122, f32[2,512]{1,0:T(2,128)S(1)} %get-tuple-element.237, f32[512,2,1024]{2,0,1:T(8,128)S(1)} %get-tuple-element.236, pred[512,1024]{1,0:T(8,128)(4,1)S(1)} %iota_compare_fusion.2, ...), kind=kOutput, calls=%fused_computation.3.clone.1 | convolution fusion | flops 274725888 | bytes 9449476 | tf_op jit(solution)/shard_map/while/body/eval_jaxpr/qgrd,kgd->grqk/dot_general | solution.py:90
  126.6 1.6 fusion.124
  128.2 2.2 fusion.125
  130.4 4.6 %fusion.126 = f32[1024,1,128]{0,2,1:T(8,128)} fusion(f32[512,2,1024]{2,0,1:T(8,128)} %copy-done.1, f32[2,512]{1,0:T(2,128)S(1)} %fusion.122, f32[2,512]{1,0:T(2,128)S(1)} %get-tuple-element.237, pred[512,1024]{1,0:T(8,128)(4,1)S(1)} %iota_compare_fusion.2, f32[1024,1,128]{0,2,1:T(8,128)} %get-tuple-element.255, pred[]{:T(512)S(6)} %compare.3, ...), kind=kOutput, calls=%fused_computation.21.clone.1 | convolution fusion | flops 273940480 | bytes 6037509 | tf_op jit(solution)/shard_map/while/body/eval_jaxpr/grqk,qgrd->kgd/dot_general | solution.py:87
  135.0 1.7 fusion.127
  139.2 2.1 fusion.121
  142.6 3.3 %fusion.123 = (f32[2,512]{1,0:T(2,128)S(1)}, f32[512,2,1024]{2,0,1:T(8,128)S(1)}) fusion(f32[2,512]{1,0:T(2,128)S(1)} %fusion.122, f32[2,512]{1,0:T(2,128)S(1)} %get-tuple-element.237, f32[512,2,1024]{2,0,1:T(8,128)S(1)} %get-tuple-element.236, pred[512,1024]{1,0:T(8,128)(4,1)S(1)} %iota_compare_fusion.2, ...), kind=kOutput, calls=%fused_computation.3.clone.1 | convolution fusion | flops 274725888 | bytes 9449476 | tf_op jit(solution)/shard_map/while/body/eval_jaxpr/qgrd,kgd->grqk/dot_general | solution.py:90
  145.9 1.6 fusion.124
  147.5 2.5 fusion.125
  150.0 4.8 %fusion.126 = f32[1024,1,128]{0,2,1:T(8,128)} fusion(f32[512,2,1024]{2,0,1:T(8,128)} %copy-done.1, f32[2,512]{1,0:T(2,128)S(1)} %fusion.122, f32[2,512]{1,0:T(2,128)S(1)} %get-tuple-element.237, pred[512,1024]{1,0:T(8,128)(4,1)S(1)} %iota_compare_fusion.2, f32[1024,1,128]{0,2,1:T(8,128)} %get-tuple-element.255, pred[]{:T(512)S(6)} %compare.3, ...), kind=kOutput, calls=%fused_computation.21.clone.1 | convolution fusion | flops 273940480 | bytes 6037509 | tf_op jit(solution)/shard_map/while/body/eval_jaxpr/grqk,qgrd->kgd/dot_general | solution.py:87
  154.8 1.7 fusion.127
  157.5 2.3 copy.64
  159.8 2.1 reshape_reshape.6
  162.1 2.7 fusion.80
  164.9 2.9 %fusion.79 = bf16[1024,1,128]{0,2,1:T(8,128)(2,1)S(1)} fusion(f32[1024,1,128]{0,2,1:T(8,128)S(1)} %copy-done.3, f32[1024,1,64]{0,2,1:T(8,128)} %get-tuple-element.175, f32[1024,1,64]{0,2,1:T(8,128)S(1)} %get-tuple-element.169, f32[1024,1,64]{0,2,1:T(8,128)S(1)} %get-tuple-element.168), kind=kLoop, calls=%fused_computation.99 | loop fusion | flops 655360 | bytes 1572864 | tf_op jit(solution)/shard_map/convert_element_type | solution.py:174
  169.2 6.4 %fusion.65 = f32[1024,3072]{1,0:T(8,128)} fusion(bf16[1,3072,128]{2,1,0:T(8,128)(2,1)S(1)} %copy-done, bf16[1024,1,128]{0,2,1:T(8,128)(2,1)S(1)} %fusion.79), kind=kOutput, calls=%fused_computation.81 | convolution fusion | flops 805306368 | bytes 13631488 | tf_op jit(solution)/shard_map/dot_general | solution.py:192
  175.5 6.4 %fusion.55 = f32[1024,3072]{1,0:T(8,128)} fusion(bf16[1024,256]{0,1:T(8,128)(2,1)S(1)} %bitcast.241, bf16[1,3072,256]{2,1,0:T(8,128)(2,1)S(1)} %copy-done.7), kind=kOutput, calls=%fused_computation.65 | convolution fusion | flops 1610612736 | bytes 14680064 | tf_op jit(solution)/shard_map/dot_general | solution.py:191
  181.9 12.0 %add_convert_fusion = bf16[1024,3072]{1,0:T(8,128)(2,1)} fusion(f32[1024,3072]{1,0:T(8,128)} %fusion.55, f32[1024,3072]{1,0:T(8,128)} %fusion.65, bf16[1,3072,128]{2,1,0:T(8,128)(2,1)S(1)} %copy-done.19, f32[1024,1,128]{0,2,1:T(8,128)S(1)} %copy-done.12), kind=kOutput, calls=%fused_computation.42 | convolution fusion | flops 814874624 | bytes 32768000 | tf_op jit(solution)/shard_map/dot_general | solution.py:198
  194.0 2.4 reshape.232
  196.4 1.3 fusion.90
  197.7 3.0 %copy.62 = f32[2,512,1,2,128]{4,3,1,0,2:T(2,128)} copy(f32[2,512,1,2,128]{4,1,3,2,0:T(8,128)} %get-tuple-element.56) | data formatting | bytes 2097152 | tf_op jit(solution)/shard_map/while | solution.py:108
  200.7 2.7 copy.65
  204.6 2.6 copy.63
  207.1 5.7 %fusion.42 = bf16[1,3072,128]{2,1,0:T(8,128)(2,1)} fusion(bf16[1024,3072]{1,0:T(8,128)(2,1)} %all-gather.4.cloned.1.call-done, bf16[1024,1,128]{0,2,1:T(8,128)(2,1)} %copy-done.14), kind=kOutput, calls=%fused_computation.49 | convolution fusion | flops 805699584 | bytes 7340032 | tf_op jit(solution)/shard_map/dot_general | solution.py:184
  212.9 2.8 fusion.43
  215.7 3.1 %fusion.41 = bf16[1,3072,256]{2,1,0:T(8,128)(2,1)} fusion(bf16[1024,3072]{1,0:T(8,128)(2,1)S(1)} %bitcast.236, f32[1024,256]{1,0:T(8,128)S(1)} %copy-done.17, f32[1024,256]{1,0:T(8,128)S(1)} %copy-done.18, f32[128,8,2,128]{3,2,1,0:T(2,128)S(1)} %bitcast.243), kind=kOutput, calls=%fused_computation.46 | convolution fusion | flops 1612185600 | bytes 11010048 | tf_op jit(solution)/shard_map/dot_general | solution.py:181
  218.8 49.4 %reduce-scatter.2.cloned.1.call-done = bf16[128,3072]{1,0:T(8,128)(2,1)} async-done(((bf16[1024,3072]{1,0:T(8,128)(2,1)}), bf16[128,3072]{1,0:T(8,128)(2,1)}) %reduce-scatter.2.cloned.1.call-update) | async-done | bytes 786448 | tf_op jit(solution)/shard_map/reduce_scatter | solution.py:195
  268.1 1.9 fusion.53
  270.8 3.4 %all-to-all-start = ((f32[8,1,3072]{2,1,0:T(1,128)}), f32[8,1,3072]{2,1,0:T(1,128)S(1)}, u32[]{:S(2)}, u32[]{:S(2)}) async-start(f32[8,1,3072]{2,1,0:T(1,128)} %broadcast_in_dim.52), calls=%async_computation.1 | async-start | bytes 196608 | tf_op jit(solution)/shard_map/all_to_all | solution.py:15
  274.1 2.7 fusion.62
  276.8 3.7 %all-to-all-done = f32[8,1,3072]{2,1,0:T(1,128)S(1)} async-done(((f32[8,1,3072]{2,1,0:T(1,128)}), f32[8,1,3072]{2,1,0:T(1,128)S(1)}, u32[]{:S(2)}, u32[]{:S(2)}) %all-to-all-start) | async-done | bytes 98336 | tf_op jit(solution)/shard_map/all_to_all | solution.py:15
  (92 shorter events, 14.7 us)
Async XLA Ops:
  7.2 96.5 %copy-start = (bf16[1,3072,128]{2,1,0:T(8,128)(2,1)S(1)}, bf16[1,3072,128]{2,1,0:T(8,128)(2,1)}, u32[]{:S(2)}) copy-start(bf16[1,3072,128]{2,1,0:T(8,128)(2,1)} %param.14) | copy-start | bytes 2359300
  7.2 18.7 %copy-start.6 = (bf16[1,3072,256]{2,1,0:T(8,128)(2,1)S(1)}, bf16[1,3072,256]{2,1,0:T(8,128)(2,1)}, u32[]{:S(2)}) copy-start(bf16[1,3072,256]{2,1,0:T(8,128)(2,1)} %param.13) | copy-start | bytes 4718596
  7.2 90.3 %all-gather.4.cloned.1.call-start = ((), (), s32[]{:S(2)}) async-start(), calls=%async_computation.3 | async-start | bytes 7077888 | tf_op jit(solution)/shard_map/all_gather | solution.py:136
  8.8 0.5 copy-start.21
  14.2 33.9 %all-to-all-start.1 = ((f32[32,2,3072]{2,1,0:T(2,128)}), f32[32,2,3072]{2,1,0:T(2,128)S(1)}, u32[]{:S(2)}, u32[]{:S(2)}) async-start(f32[32,2,3072]{2,1,0:T(2,128)} %reshape.228), calls=%async_computation.2 | async-start | bytes 1572864 | tf_op jit(solution)/shard_map/all_to_all | solution.py:30
  25.8 168.2 %all-gather.6.cloned.1.call-start = ((), (), s32[]{:S(2)}) async-start(), calls=%async_computation.5 | async-start | bytes 1622016 | tf_op jit(solution)/shard_map/all_gather | solution.py:36
  50.1 218.1 %reduce-scatter.2.cloned.1.call-start = ((), (), s32[]{:S(2)}) async-start(), calls=%async_computation.4 | async-start | bytes 7077888 | tf_op jit(solution)/shard_map/reduce_scatter | solution.py:195
  97.5 6.1 %copy-start.2 = (bf16[1024,3072]{1,0:T(8,128)(2,1)S(1)}, bf16[1024,3072]{1,0:T(8,128)(2,1)}, u32[]{:S(2)}) copy-start(bf16[1024,3072]{1,0:T(8,128)(2,1)} %all-gather.4.cloned.1.call-done) | copy-start | bytes 18874372
  103.6 2.3 copy-start.15
  108.8 9.6 %copy-start.4 = (f32[1024,128]{0,1:T(8,128)}, f32[1024,128]{0,1:T(8,128)S(1)}, u32[]{:S(2)}) copy-start(f32[1024,128]{0,1:T(8,128)S(1)} %get-tuple-element.174) | copy-start | bytes 1572868
  108.8 9.6 %copy-start.8 = (f32[1024,128]{0,1:T(8,128)}, f32[1024,128]{0,1:T(8,128)S(1)}, u32[]{:S(2)}) copy-start(f32[1024,128]{0,1:T(8,128)S(1)} %get-tuple-element.173) | copy-start | bytes 1572868
  122.1 4.5 %copy-start.1 = (f32[512,2,1024]{2,0,1:T(8,128)}, f32[512,2,1024]{2,0,1:T(8,128)S(1)}, u32[]{:S(2)}) copy-start(f32[512,2,1024]{2,0,1:T(8,128)S(1)} %get-tuple-element.236) | copy-start | bytes 12582916 | tf_op jit(solution)/shard_map/while
  130.4 4.6 %copy-start.10 = (f32[2,512,1,2,128]{4,1,3,2,0:T(8,128)S(1)}, f32[2,512,1,2,128]{4,1,3,2,0:T(8,128)}, u32[]{:S(2)}) copy-start(f32[2,512,1,2,128]{4,1,3,2,0:T(8,128)} %get-tuple-element.256) | copy-start | bytes 3145732 | tf_op jit(solution)/shard_map/while
  136.7 1.0 copy-start.11
  141.4 4.5 %copy-start.1 = (f32[512,2,1024]{2,0,1:T(8,128)}, f32[512,2,1024]{2,0,1:T(8,128)S(1)}, u32[]{:S(2)}) copy-start(f32[512,2,1024]{2,0,1:T(8,128)S(1)} %get-tuple-element.236) | copy-start | bytes 12582916 | tf_op jit(solution)/shard_map/while
  150.0 4.8 %copy-start.10 = (f32[2,512,1,2,128]{4,1,3,2,0:T(8,128)S(1)}, f32[2,512,1,2,128]{4,1,3,2,0:T(8,128)}, u32[]{:S(2)}) copy-start(f32[2,512,1,2,128]{4,1,3,2,0:T(8,128)} %get-tuple-element.256) | copy-start | bytes 3145732 | tf_op jit(solution)/shard_map/while
  156.4 1.0 copy-start.11
  157.5 4.5 %copy-start.9 = (f32[1024,128]{0,1:T(8,128)S(1)}, f32[1024,128]{0,1:T(8,128)}, u32[]{:S(2)}) copy-start(f32[1024,128]{0,1:T(8,128)} %copy-done.8) | copy-start | bytes 1572868
  157.5 4.6 %copy-start.3 = (f32[1024,1,128]{0,2,1:T(8,128)S(1)}, f32[1024,1,128]{0,2,1:T(8,128)}, u32[]{:S(2)}) copy-start(f32[1024,1,128]{0,2,1:T(8,128)} %get-tuple-element.57) | copy-start | bytes 1572868
  161.9 6.0 %copy-start.5 = (f32[1024,128]{0,1:T(8,128)S(1)}, f32[1024,128]{0,1:T(8,128)}, u32[]{:S(2)}) copy-start(f32[1024,128]{0,1:T(8,128)} %copy-done.4) | copy-start | bytes 1572868
  167.8 7.7 %copy-start.14 = (bf16[1024,1,128]{0,2,1:T(8,128)(2,1)}, bf16[1024,1,128]{0,2,1:T(8,128)(2,1)S(1)}, u32[]{:S(2)}) copy-start(bf16[1024,1,128]{0,2,1:T(8,128)(2,1)S(1)} %fusion.79) | copy-start | bytes 786436
  169.2 6.4 %copy-start.7 = (bf16[1,3072,256]{2,1,0:T(8,128)(2,1)S(1)}, bf16[1,3072,256]{2,1,0:T(8,128)(2,1)}, u32[]{:S(2)}) copy-start(bf16[1,3072,256]{2,1,0:T(8,128)(2,1)} %param.13) | copy-start | bytes 4718596
  175.5 6.4 %copy-start.12 = (f32[1024,1,128]{0,2,1:T(8,128)S(1)}, f32[1024,1,128]{0,2,1:T(8,128)}, u32[]{:S(2)}) copy-start(f32[1024,1,128]{0,2,1:T(8,128)} %get-tuple-element.58) | copy-start | bytes 1572868
  175.5 6.4 %copy-start.19 = (bf16[1,3072,128]{2,1,0:T(8,128)(2,1)S(1)}, bf16[1,3072,128]{2,1,0:T(8,128)(2,1)}, u32[]{:S(2)}) copy-start(bf16[1,3072,128]{2,1,0:T(8,128)(2,1)} %param.15) | copy-start | bytes 2359300
  200.7 12.1 %slice-start = ((s8[6291456]{0:T(1024)(128)(4,1)}), s8[2097152]{0:T(1024)(128)(4,1)S(1)}, s32[]{:S(2)}) async-start(s8[6291456]{0:T(1024)(128)(4,1)} %bitcast.235), calls=%async_computation.6 | async-start | bytes 4194304
  207.1 5.7 %slice-start.1 = ((s8[6291456]{0:T(1024)(128)(4,1)}), s8[4194304]{0:T(1024)(128)(4,1)S(1)}, s32[]{:S(2)}) async-start(s8[6291456]{0:T(1024)(128)(4,1)} %bitcast.235), calls=%async_computation.7 | async-start | bytes 8388608
  207.1 5.7 %copy-start.13 = (f32[1024,1,128]{0,2,1:T(8,128)S(1)}, f32[1024,1,128]{0,2,1:T(8,128)}, u32[]{:S(2)}) copy-start(f32[1024,1,128]{0,2,1:T(8,128)} %get-tuple-element.58) | copy-start | bytes 1572868
  212.8 2.8 copy-start.16
  212.8 2.8 copy-start.17
  212.9 2.8 copy-start.18
  215.6 52.5 %copy-start.20 = (f32[1,3072]{1,0:T(1,128)S(1)}, f32[1,3072]{1,0:T(1,128)}, u32[]{:S(2)}) copy-start(f32[1,3072]{1,0:T(1,128)} %param.12) | copy-start | bytes 36868
  215.6 52.5 %copy-start.22 = (f32[128]{0:T(128)S(1)}, f32[128]{0:T(128)}, u32[]{:S(2)}) copy-start(f32[128]{0:T(128)} %copy-done.21) | copy-start | bytes 1540
  270.8 9.7 %all-to-all-start = ((f32[8,1,3072]{2,1,0:T(1,128)}), f32[8,1,3072]{2,1,0:T(1,128)S(1)}, u32[]{:S(2)}, u32[]{:S(2)}) async-start(f32[8,1,3072]{2,1,0:T(1,128)} %broadcast_in_dim.52), calls=%async_computation.1 | async-start | bytes 196608 | tf_op jit(solution)/shard_map/all_to_all | solution.py:15
Sparse Core Ops, SparseCore 0:
  11.7 85.7 all-gather.3
  100.3 75.0 all-gather.5
  194.1 73.9 reduce-scatter.1
where the time goes:
time: 289 us; the launch traced here: 288 us
  waiting for transfers between devices  118 us (41%)
  matrix products  77.4 us (27%)
  other arithmetic  32.6 us (11%)
  local copies, waits for them, and re-layouts  29.2 us (10%)
  starting transfers between devices  15.1 us (5%)
  between operations  14 us (5%)
    reduce_scatter x1, waiting for transfers between devices, body(): lax.psum_scatter((partial_value + lax.dot_general(value_gradient, weight_...  49.4 us
    all_gather x1, waiting for transfers between devices, body(): normalized = lax.all_gather(normalized_local, 'tp', axis=0, tiled=True)  47.4 us
    all_to_all x1, waiting for transfers between devices, sent_and_summed(): lax.all_to_all(parts, axis, split_axis=0, concat_axis=0, tiled=True)  17.6 us
    dot_general x1, matrix products, body(): lax.dot_general(value_gradient, weight_v, back, preferred_element_type=jn...  12 us
    all_to_all x1, starting transfers between devices, sent_and_summed(): lax.all_to_all(parts, axis, split_axis=0, concat_axis=0, tiled=True)  11.6 us
    dot_general x2, matrix products, one_block(): jnp.einsum('grqk,qgrd->kgd', prob_low, grad_block, preferred_element_type...  9.39 us
    unnamed x47, local copies, waits for them, and re-layouts  7 us
    dot_general x2, matrix products, one_block(): jnp.einsum('qgrd,kgd->grqk', grad_block, values_bfloat, preferred_element...  6.59 us
  transfers between devices with their start and end apart: 5, of which 4 were waited for; matrix products, arithmetic and copies ran while one was open for 45% of the time, Pallas kernels for 0%

commit v1 on v0

--- a/solution.py
+++ b/solution.py
@@ -133,7 +133,9 @@
     )
     normalized_input = widened_rows * inverse_norm
     normalized_local = (normalized_input * norm_gains[None, :]).astype(jnp.bfloat16)
-    normalized = lax.all_gather(normalized_local, "tp", axis=0, tiled=True)
+    normalized = jnp.concatenate(
+        lax.all_to_all(jnp.stack([normalized_local] * lax.axis_size("tp")), "tp", 0, 0), axis=0
+    )
     sequence_length = normalized.shape[0]
     heads_q = weight_q.shape[1] // HEAD_SIZE
     heads_kv = weight_k.shape[1] // HEAD_SIZE

time: 289 us -> 338 us (1.17)
  waiting for transfers between devices: 118 us -> 144 us
  local copies, waits for them, and re-layouts: 29.2 us -> 42.4 us
  matrix products: 77.4 us -> 85.6 us
  other arithmetic: 32.6 us -> 26.1 us
  starting transfers between devices: 15.1 us -> 20.3 us
    all_to_all x0 -> x1, waiting for transfers between devices: none -> 67 us  [body(): lax.all_to_all(jnp.stack([normalized_local] * lax.axis_size('tp')), 'tp',...]
    all_gather x1 -> x0, waiting for transfers between devices: 47.4 us -> none  [body(): normalized = lax.all_gather(normalized_local, 'tp', axis=0, tiled=True)]
    dynamic_update_slice x0 -> x4, local copies, waits for them, and re-layouts: none -> 23.2 us  [attention_reverse(): lax.scan(one_block, (initial, initial), jnp.arange(sequence_length // blo...]
    while x14 -> x12, local copies, waits for them, and re-layouts: 7.43 us -> 0.03 us  [the longest x2 5.39 us: attention_reverse(): lax.scan(one_block, (initial, initial), jnp.arange(sequence_length // blo...]
    all_to_all x0 -> x1, starting transfers between devices: none -> 5.24 us  [body(): lax.all_to_all(jnp.stack([normalized_local] * lax.axis_size('tp')), 'tp',...]
    all_to_all x1, waiting for transfers between devices: 17.6 us -> 21.3 us  [sent_and_summed(): lax.all_to_all(parts, axis, split_axis=0, concat_axis=0, tiled=True)]
    mul x2 -> x0, local copies, waits for them, and re-layouts: 3.68 us -> none  [rotate(): return vectors * cosine_table + turned * sine_table]
    another operation x0 -> x1, local copies, waits for them, and re-layouts: none -> 3.46 us  [body(): jnp.stack([normalized_local] * lax.axis_size('tp'))]
  transfers between devices with their start and end apart: 5 -> 5, of which waited for: 4 -> 4; matrix products, arithmetic and copies ran while one was open for 45% -> 43% of each run, Pallas kernels for 0% -> 0%
where the time goes in v1:
time: 338 us; the launch traced here: 336 us
  waiting for transfers between devices  144 us (43%)
  matrix products  85.6 us (25%)
  local copies, waits for them, and re-layouts  42.4 us (13%)
  other arithmetic  26.1 us (8%)
  starting transfers between devices  20.3 us (6%)
  between operations  15.8 us (5%)
    all_to_all x1, waiting for transfers between devices, body(): lax.all_to_all(jnp.stack([normalized_local] * lax.axis_size('tp')), 'tp',...  67 us
    reduce_scatter x1, waiting for transfers between devices, body(): lax.psum_scatter((partial_value + lax.dot_general(value_gradient, weight_...  52.2 us
    dynamic_update_slice x4, local copies, waits for them, and re-layouts, attention_reverse(): lax.scan(one_block, (initial, initial), jnp.arange(sequence_length // blo...  23.2 us
    all_to_all x1, waiting for transfers between devices, sent_and_summed(): lax.all_to_all(parts, axis, split_axis=0, concat_axis=0, tiled=True)  21.3 us
    dot_general x1, matrix products, body(): lax.dot_general(value_gradient, weight_v, back, preferred_element_type=jn...  12.2 us
    all_to_all x1, starting transfers between devices, sent_and_summed(): lax.all_to_all(parts, axis, split_axis=0, concat_axis=0, tiled=True)  11.6 us
    dot_general x2, matrix products, one_block(): jnp.einsum('grqk,qgrd->kgd', prob_low, grad_block, preferred_element_type...  9.23 us
    unnamed x41, local copies, waits for them, and re-layouts  7.23 us
  transfers between devices with their start and end apart: 5, of which 4 were waited for; matrix products, arithmetic and copies ran while one was open for 43% of the time, Pallas kernels for 0%

profile of v1, /device:TPU:4, one launch (start us, length us, event | category | flops | bytes accessed | tf_op | source)
XLA Modules:
  0.0 336.0 jit_solution(15318625140847735175)
XLA Ops:
  8.0 1.4 convert_subtract_fusion
  9.5 1.3 reshape.254
  10.8 11.6 %all-to-all-start.2 = ((f32[32,2,3072]{2,1,0:T(2,128)}), f32[32,2,3072]{2,1,0:T(2,128)S(1)}, u32[]{:S(2)}, u32[]{:S(2)}) async-start(f32[32,2,3072]{2,1,0:T(2,128)} %reshape.254), calls=%async_computation.3 | async-start | bytes 1572864 | tf_op jit(solution)/shard_map/all_to_all | solution.py:30
  23.4 21.3 %all-to-all-done.2 = f32[32,2,3072]{2,1,0:T(2,128)S(1)} async-done(((f32[32,2,3072]{2,1,0:T(2,128)}), f32[32,2,3072]{2,1,0:T(2,128)S(1)}, u32[]{:S(2)}, u32[]{:S(2)}) %all-to-all-start.2) | async-done | bytes 786464 | tf_op jit(solution)/shard_map/all_to_all | solution.py:30
  44.7 3.5 %stack.5 = bf16[8,128,3072]{2,1,0:T(8,128)(2,1)} broadcast(bf16[128,3072]{1,0:T(8,128)(2,1)S(1)} %fusion.59), dimensions={1,2} | broadcast | bytes 7077888 | tf_op jit(solution)/shard_map/stack | solution.py:137
  48.2 5.2 %all-to-all-start = ((bf16[8,128,3072]{2,1,0:T(8,128)(2,1)}), bf16[8,128,3072]{2,1,0:T(8,128)(2,1)}, u32[]{:S(2)}, u32[]{:S(2)}) async-start(bf16[8,128,3072]{2,1,0:T(8,128)(2,1)} %stack.5), calls=%async_computation | async-start | bytes 12582912 | tf_op jit(solution)/shard_map/all_to_all | solution.py:137
  53.5 1.7 copy.57
  55.3 2.0 copy.49
  60.1 67.0 %all-to-all-done = bf16[8,128,3072]{2,1,0:T(8,128)(2,1)} async-done(((bf16[8,128,3072]{2,1,0:T(8,128)(2,1)}), bf16[8,128,3072]{2,1,0:T(8,128)(2,1)}, u32[]{:S(2)}, u32[]{:S(2)}) %all-to-all-start) | async-done | bytes 6291488 | tf_op jit(solution)/shard_map/all_to_all | solution.py:137
  127.1 5.0 %fusion.90 = f32[1024,2,128]{0,2,1:T(8,128)S(1)} fusion(bf16[1024,3072,1]{1,0,2:T(8,128)(2,1)} %bitcast.4, bf16[2,128,3072]{2,1,0:T(8,128)(2,1)} %bitcast.244), kind=kOutput, calls=%fused_computation.121 | convolution fusion | flops 1610612736 | bytes 8912896 | tf_op jit(solution)/shard_map/dot_general | solution.py:143
  133.1 5.1 %fusion.65 = f32[1024,128]{0,1:T(8,128)S(1)} fusion(bf16[1024,3072]{1,0:T(8,128)(2,1)} %bitcast.3, bf16[1,3072,128]{2,1,0:T(8,128)(2,1)S(1)} %copy-done), kind=kOutput, calls=%fused_computation.80 | convolution fusion | flops 805306368 | bytes 7602176 | tf_op jit(solution)/shard_map/dot_general | solution.py:147
  138.2 2.9 fusion.78
  141.1 2.0 copy.51
  143.1 5.5 %fusion.55 = bf16[1024,1,128]{2,0,1:T(8,128)(2,1)} fusion(bf16[1024,3072]{1,0:T(8,128)(2,1)} %bitcast.3, bf16[1,3072,128]{2,1,0:T(8,128)(2,1)} %param.15), kind=kOutput, calls=%fused_computation.67 | convolution fusion | flops 805437440 | bytes 7340032 | tf_op jit(solution)/shard_map/dot_general | solution.py:152
  149.7 59.9 %while.15 = (s32[]{:T(128)}, f32[1024,1,128]{0,2,1:T(8,128)}, f32[1024,1,128]{0,2,1:T(8,128)}, f32[2,512,1,2,128]{1,0,4,3,2:T(2,128)}, s32[2]{0:T(128)S(1)}, /*i...) while((s32[]{:T(128)}, f32[1024,1,128]{0,2,1:T(8,128)}, ...), condition=%wide.region_5.6_spmd.clone, body=%wide.region_1.5_spmd.clone.sunk | while | flops 1370486272 | bytes 65323312 | solution.py:108
  151.4 2.2 fusion.120
  154.8 2.3 fusion.122
  157.1 1.6 fusion.123
  158.7 2.2 fusion.124
  160.9 4.6 %fusion.125 = f32[1024,1,128]{0,2,1:T(8,128)} fusion(f32[512,2,1024]{2,0,1:T(8,128)} %copy-done.1, f32[2,512]{1,0:T(2,128)S(1)} %fusion.121, f32[2,512]{1,0:T(2,128)S(1)} %get-tuple-element.235, pred[512,1024]{1,0:T(8,128)(4,1)S(1)} %iota_compare_fusion.2, f32[1024,1,128]{0,2,1:T(8,128)} %get-tuple-element.253, pred[]{:T(512)S(6)} %compare.3, ...), kind=kOutput, calls=%fused_computation.20.clone.1 | convolution fusion | flops 273940480 | bytes 6037509 | tf_op jit(solution)/shard_map/while/body/eval_jaxpr/grqk,qgrd->kgd/dot_general | solution.py:87
  165.5 2.5 convolution_bitcast_fusion.3
  167.9 1.3 copy.69
  169.2 10.3 %dynamic_update_slice.6 = f32[2,512,1,2,128]{1,0,4,3,2:T(2,128)} dynamic-update-slice(f32[2,512,1,2,128]{1,0,4,3,2:T(2,128)} %get-tuple-element.254, f32[1,512,1,2,128]{1,0,4,3,2:T(1,128)S(1)} %copy.69, s32[]{:T(128)S(6)} %copy.75, s32[]{:T(128)} %constant.32.clone.1..sunk, s32[]{:T(128)} %constant.32.clone.1..sunk, s32[]{:T(128)} %constant.32.clone.1..sunk, s32[]{:T(128)} %constant.32.clone.1..sunk) | dynamic-update-slice | bytes 1048580 | tf_op jit(solution)/shard_map/while/body/jit(dynamic_update_index_in_dim)/dynamic_update_slice | solution.py:108
  181.2 2.2 fusion.120
  184.6 2.3 fusion.122
  186.9 1.6 fusion.123
  188.5 2.4 fusion.124
  190.9 4.7 %fusion.125 = f32[1024,1,128]{0,2,1:T(8,128)} fusion(f32[512,2,1024]{2,0,1:T(8,128)} %copy-done.1, f32[2,512]{1,0:T(2,128)S(1)} %fusion.121, f32[2,512]{1,0:T(2,128)S(1)} %get-tuple-element.235, pred[512,1024]{1,0:T(8,128)(4,1)S(1)} %iota_compare_fusion.2, f32[1024,1,128]{0,2,1:T(8,128)} %get-tuple-element.253, pred[]{:T(512)S(6)} %compare.3, ...), kind=kOutput, calls=%fused_computation.20.clone.1 | convolution fusion | flops 273940480 | bytes 6037509 | tf_op jit(solution)/shard_map/while/body/eval_jaxpr/grqk,qgrd->kgd/dot_general | solution.py:87
  195.5 2.5 convolution_bitcast_fusion.3
  198.0 1.3 copy.69
  199.3 10.3 %dynamic_update_slice.6 = f32[2,512,1,2,128]{1,0,4,3,2:T(2,128)} dynamic-update-slice(f32[2,512,1,2,128]{1,0,4,3,2:T(2,128)} %get-tuple-element.254, f32[1,512,1,2,128]{1,0,4,3,2:T(1,128)S(1)} %copy.69, s32[]{:T(128)S(6)} %copy.75, s32[]{:T(128)} %constant.32.clone.1..sunk, s32[]{:T(128)} %constant.32.clone.1..sunk, s32[]{:T(128)} %constant.32.clone.1..sunk, s32[]{:T(128)} %constant.32.clone.1..sunk) | dynamic-update-slice | bytes 1048580 | tf_op jit(solution)/shard_map/while/body/jit(dynamic_update_index_in_dim)/dynamic_update_slice | solution.py:108
  209.6 2.2 reshape_reshape.3
  211.8 1.2 broadcast_multiply_fusion
  213.1 1.7 fusion.77
  214.9 2.0 fusion.76
  217.2 6.3 %fusion.63 = f32[1024,3072]{1,0:T(8,128)} fusion(bf16[1,3072,128]{2,1,0:T(8,128)(2,1)S(1)} %copy-done, bf16[1024,1,128]{0,2,1:T(8,128)(2,1)S(1)} %fusion.76), kind=kOutput, calls=%fused_computation.78 | convolution fusion | flops 805306368 | bytes 13631488 | tf_op jit(solution)/shard_map/dot_general | solution.py:194
  223.6 6.4 %fusion.53 = f32[1024,3072]{1,0:T(8,128)} fusion(bf16[1024,256]{0,1:T(8,128)(2,1)S(1)} %bitcast.242, bf16[1,3072,256]{2,1,0:T(8,128)(2,1)S(1)} %copy-done.6), kind=kOutput, calls=%fused_computation.64 | convolution fusion | flops 1610612736 | bytes 14680064 | tf_op jit(solution)/shard_map/dot_general | solution.py:193
  230.0 12.2 %add_convert_fusion = bf16[1024,3072]{1,0:T(8,128)(2,1)} fusion(f32[1024,3072]{1,0:T(8,128)} %fusion.53, f32[1024,3072]{1,0:T(8,128)} %fusion.63, bf16[1,3072,128]{2,1,0:T(8,128)(2,1)S(1)} %copy-done.15, f32[1024,1,128]{0,2,1:T(8,128)S(1)} %copy-done.11), kind=kOutput, calls=%fused_computation.41 | convolution fusion | flops 814874624 | bytes 32768000 | tf_op jit(solution)/shard_map/dot_general | solution.py:200
  242.2 2.7 reshape.258
  244.9 1.3 fusion.87
  246.2 5.5 %fusion.39 = bf16[1,3072,128]{2,1,0:T(8,128)(2,1)} fusion(bf16[1024,3072]{1,0:T(8,128)(2,1)} %bitcast.3, bf16[1024,1,128]{0,2,1:T(8,128)(2,1)} %copy-done.13), kind=kOutput, calls=%fused_computation.46 | convolution fusion | flops 805699584 | bytes 7340032 | tf_op jit(solution)/shard_map/dot_general | solution.py:186
  251.7 5.9 %fusion.40 = bf16[1,3072,128]{2,1,0:T(8,128)(2,1)} fusion(bf16[1024,3072]{1,0:T(8,128)(2,1)} %bitcast.3, f32[1024,1,128]{0,2,1:T(8,128)S(1)} %copy-done.11), kind=kOutput, calls=%fused_computation.47 | convolution fusion | flops 805830656 | bytes 7602176 | tf_op jit(solution)/shard_map/dot_general | solution.py:189
  257.6 6.0 %fusion.38 = bf16[1,3072,256]{2,1,0:T(8,128)(2,1)} fusion(bf16[1024,3072]{1,0:T(8,128)(2,1)} %bitcast.3, bf16[1024,256]{0,1:T(8,128)(2,1)S(1)} %bitcast.243), kind=kOutput, calls=%fused_computation.43 | convolution fusion | flops 1611399168 | bytes 8388608 | tf_op jit(solution)/shard_map/dot_general | solution.py:183
  263.5 52.2 %reduce-scatter.2.cloned.1.call-done = bf16[128,3072]{1,0:T(8,128)(2,1)} async-done(((bf16[1024,3072]{1,0:T(8,128)(2,1)}), bf16[128,3072]{1,0:T(8,128)(2,1)}) %reduce-scatter.2.cloned.1.call-update) | async-done | bytes 786448 | tf_op jit(solution)/shard_map/reduce_scatter | solution.py:197
  315.8 1.7 fusion.48
  318.1 3.4 %all-to-all-start.1 = ((f32[8,1,3072]{2,1,0:T(1,128)}), f32[8,1,3072]{2,1,0:T(1,128)S(1)}, u32[]{:S(2)}, u32[]{:S(2)}) async-start(f32[8,1,3072]{2,1,0:T(1,128)} %broadcast_in_dim.52), calls=%async_computation.2 | async-start | bytes 196608 | tf_op jit(solution)/shard_map/all_to_all | solution.py:15
  321.5 2.5 fusion.60
  324.0 3.9 %all-to-all-done.1 = f32[8,1,3072]{2,1,0:T(1,128)S(1)} async-done(((f32[8,1,3072]{2,1,0:T(1,128)}), f32[8,1,3072]{2,1,0:T(1,128)S(1)}, u32[]{:S(2)}, u32[]{:S(2)}) %all-to-all-start.1) | async-done | bytes 98336 | tf_op jit(solution)/shard_map/all_to_all | solution.py:15
  (84 shorter events, 12.2 us)
Async XLA Ops:
  8.0 125.1 %copy-start = (bf16[1,3072,128]{2,1,0:T(8,128)(2,1)S(1)}, bf16[1,3072,128]{2,1,0:T(8,128)(2,1)}, u32[]{:S(2)}) copy-start(bf16[1,3072,128]{2,1,0:T(8,128)(2,1)} %param.14) | copy-start | bytes 2359300
  8.0 14.4 %copy-start.3 = (bf16[1,128,3072]{2,1,0:T(8,128)(2,1)S(1)}, bf16[1,128,3072]{2,1,0:T(8,128)(2,1)}, u32[]{:S(2)}) copy-start(bf16[1,128,3072]{2,1,0:T(8,128)(2,1)} %param.11) | copy-start | bytes 2359300
  8.0 15.1 %copy-start.17 = (f32[1,3072]{1,0:T(1,128)S(1)}, f32[1,3072]{1,0:T(1,128)}, u32[]{:S(2)}) copy-start(f32[1,3072]{1,0:T(1,128)} %param.12) | copy-start | bytes 36868
  10.8 33.9 %all-to-all-start.2 = ((f32[32,2,3072]{2,1,0:T(2,128)}), f32[32,2,3072]{2,1,0:T(2,128)S(1)}, u32[]{:S(2)}, u32[]{:S(2)}) async-start(f32[32,2,3072]{2,1,0:T(2,128)} %reshape.254), calls=%async_computation.3 | async-start | bytes 1572864 | tf_op jit(solution)/shard_map/all_to_all | solution.py:30
  22.7 0.5 copy-start.19
  48.2 5.3 %copy-start.5 = (bf16[1,3072,256]{2,1,0:T(8,128)(2,1)S(1)}, bf16[1,3072,256]{2,1,0:T(8,128)(2,1)}, u32[]{:S(2)}) copy-start(bf16[1,3072,256]{2,1,0:T(8,128)(2,1)} %param.13) | copy-start | bytes 4718596
  48.2 78.9 %all-to-all-start = ((bf16[8,128,3072]{2,1,0:T(8,128)(2,1)}), bf16[8,128,3072]{2,1,0:T(8,128)(2,1)}, u32[]{:S(2)}, u32[]{:S(2)}) async-start(bf16[8,128,3072]{2,1,0:T(8,128)(2,1)} %stack.5), calls=%async_computation | async-start | bytes 12582912 | tf_op jit(solution)/shard_map/all_to_all | solution.py:137
  53.4 188.8 %all-gather.3.cloned.1.call-start = ((), (), s32[]{:S(2)}) async-start(), calls=%async_computation.5 | async-start | bytes 1622016 | tf_op jit(solution)/shard_map/all_gather | solution.py:36
  60.1 255.7 %reduce-scatter.2.cloned.1.call-start = ((), (), s32[]{:S(2)}) async-start(), calls=%async_computation.4 | async-start | bytes 7077888 | tf_op jit(solution)/shard_map/reduce_scatter | solution.py:197
  133.1 5.1 %copy-start.14 = (f32[1024,64]{0,1:T(8,128)S(1)}, f32[1024,64]{0,1:T(8,128)}, u32[]{:S(2)}) copy-start(f32[1024,64]{0,1:T(8,128)} %get-tuple-element.174) | copy-start | bytes 786436
  141.1 7.5 %copy-start.7 = (f32[1024,128]{0,1:T(8,128)}, f32[1024,128]{0,1:T(8,128)S(1)}, u32[]{:S(2)}) copy-start(f32[1024,128]{0,1:T(8,128)S(1)} %get-tuple-element.171) | copy-start | bytes 1572868
  141.1 7.5 %copy-start.8 = (f32[1024,128]{0,1:T(8,128)}, f32[1024,128]{0,1:T(8,128)S(1)}, u32[]{:S(2)}) copy-start(f32[1024,128]{0,1:T(8,128)S(1)} %get-tuple-element.172) | copy-start | bytes 1572868
  143.1 5.5 %copy-start.12 = (f32[1024,2,64]{0,2,1:T(8,128)S(1)}, f32[1024,2,64]{0,2,1:T(8,128)}, u32[]{:S(2)}) copy-start(f32[1024,2,64]{0,2,1:T(8,128)} %get-tuple-element.163) | copy-start | bytes 1572868
  151.4 3.4 %copy-start.16 = (bf16[1024,1,2,128]{0,3,2,1:T(8,128)(2,1)S(1)}, bf16[1024,1,2,128]{0,3,2,1:T(8,128)(2,1)}, u32[]{:S(2)}) copy-start(bf16[1024,1,2,128]{0,3,2,1:T(8,128)(2,1)} %get-tuple-element.271) | copy-start | bytes 1572868 | tf_op jit(solution)/shard_map/while
  151.4 3.4 %copy-start.21 = (bf16[1024,1,128]{2,0,1:T(8,128)(2,1)S(1)}, bf16[1024,1,128]{2,0,1:T(8,128)(2,1)}, u32[]{:S(2)}) copy-start(bf16[1024,1,128]{2,0,1:T(8,128)(2,1)} %get-tuple-element.272) | copy-start | bytes 786436 | tf_op jit(solution)/shard_map/while
  153.6 3.5 %copy-start.1 = (f32[512,2,1024]{2,0,1:T(8,128)}, f32[512,2,1024]{2,0,1:T(8,128)S(1)}, u32[]{:S(2)}) copy-start(f32[512,2,1024]{2,0,1:T(8,128)S(1)} %get-tuple-element.234) | copy-start | bytes 12582916 | tf_op jit(solution)/shard_map/while
  181.2 3.4 %copy-start.16 = (bf16[1024,1,2,128]{0,3,2,1:T(8,128)(2,1)S(1)}, bf16[1024,1,2,128]{0,3,2,1:T(8,128)(2,1)}, u32[]{:S(2)}) copy-start(bf16[1024,1,2,128]{0,3,2,1:T(8,128)(2,1)} %get-tuple-element.271) | copy-start | bytes 1572868 | tf_op jit(solution)/shard_map/while
  181.2 3.4 %copy-start.21 = (bf16[1024,1,128]{2,0,1:T(8,128)(2,1)S(1)}, bf16[1024,1,128]{2,0,1:T(8,128)(2,1)}, u32[]{:S(2)}) copy-start(bf16[1024,1,128]{2,0,1:T(8,128)(2,1)} %get-tuple-element.272) | copy-start | bytes 786436 | tf_op jit(solution)/shard_map/while
  183.4 3.5 %copy-start.1 = (f32[512,2,1024]{2,0,1:T(8,128)}, f32[512,2,1024]{2,0,1:T(8,128)S(1)}, u32[]{:S(2)}) copy-start(f32[512,2,1024]{2,0,1:T(8,128)S(1)} %get-tuple-element.234) | copy-start | bytes 12582916 | tf_op jit(solution)/shard_map/while
  209.6 3.4 %copy-start.2 = (f32[1024,1,128]{0,2,1:T(8,128)S(1)}, f32[1024,1,128]{0,2,1:T(8,128)}, u32[]{:S(2)}) copy-start(f32[1024,1,128]{0,2,1:T(8,128)} %get-tuple-element.57) | copy-start | bytes 1572868
  209.6 3.4 %copy-start.10 = (f32[1024,1,64]{0,2,1:T(8,128)S(1)}, f32[1024,1,64]{0,2,1:T(8,128)}, u32[]{:S(2)}) copy-start(f32[1024,1,64]{0,2,1:T(8,128)} %get-tuple-element.173) | copy-start | bytes 786436
  211.8 5.2 %copy-start.9 = (f32[1024,128]{0,1:T(8,128)S(1)}, f32[1024,128]{0,1:T(8,128)}, u32[]{:S(2)}) copy-start(f32[1024,128]{0,1:T(8,128)} %copy-done.8) | copy-start | bytes 1572868
  216.8 6.7 %copy-start.13 = (bf16[1024,1,128]{0,2,1:T(8,128)(2,1)}, bf16[1024,1,128]{0,2,1:T(8,128)(2,1)S(1)}, u32[]{:S(2)}) copy-start(bf16[1024,1,128]{0,2,1:T(8,128)(2,1)S(1)} %fusion.76) | copy-start | bytes 786436
  217.2 6.4 %copy-start.6 = (bf16[1,3072,256]{2,1,0:T(8,128)(2,1)S(1)}, bf16[1,3072,256]{2,1,0:T(8,128)(2,1)}, u32[]{:S(2)}) copy-start(bf16[1,3072,256]{2,1,0:T(8,128)(2,1)} %param.13) | copy-start | bytes 4718596
  223.6 6.4 %copy-start.11 = (f32[1024,1,128]{0,2,1:T(8,128)S(1)}, f32[1024,1,128]{0,2,1:T(8,128)}, u32[]{:S(2)}) copy-start(f32[1024,1,128]{0,2,1:T(8,128)} %get-tuple-element.58) | copy-start | bytes 1572868
  223.6 6.4 %copy-start.15 = (bf16[1,3072,128]{2,1,0:T(8,128)(2,1)S(1)}, bf16[1,3072,128]{2,1,0:T(8,128)(2,1)}, u32[]{:S(2)}) copy-start(bf16[1,3072,128]{2,1,0:T(8,128)(2,1)} %param.15) | copy-start | bytes 2359300
  257.6 58.2 %copy-start.4 = (bf16[1,128,3072]{2,1,0:T(8,128)(2,1)S(1)}, bf16[1,128,3072]{2,1,0:T(8,128)(2,1)}, u32[]{:S(2)}) copy-start(bf16[1,128,3072]{2,1,0:T(8,128)(2,1)} %param.11) | copy-start | bytes 2359300
  257.6 58.2 %copy-start.18 = (f32[1,3072]{1,0:T(1,128)S(1)}, f32[1,3072]{1,0:T(1,128)}, u32[]{:S(2)}) copy-start(f32[1,3072]{1,0:T(1,128)} %param.12) | copy-start | bytes 36868
  257.6 58.2 %copy-start.20 = (f32[128]{0:T(128)S(1)}, f32[128]{0:T(128)}, u32[]{:S(2)}) copy-start(f32[128]{0:T(128)} %copy-done.19) | copy-start | bytes 1540
  318.1 9.7 %all-to-all-start.1 = ((f32[8,1,3072]{2,1,0:T(1,128)}), f32[8,1,3072]{2,1,0:T(1,128)S(1)}, u32[]{:S(2)}, u32[]{:S(2)}) async-start(f32[8,1,3072]{2,1,0:T(1,128)} %broadcast_in_dim.52), calls=%async_computation.2 | async-start | bytes 196608 | tf_op jit(solution)/shard_map/all_to_all | solution.py:15
Sparse Core Ops, SparseCore 0:
  60.2 77.8 all-gather.2
Sparse Core Ops, SparseCore 1:
  242.3 73.4 reduce-scatter.1
